TPU v7x, 512 devices: a whole 4x8x8 slice. The times are simulated.
512 devices in a mesh: batch: 64 (over z, y), cols: 8 (over x, core).
Axes of the slice: x: 4, y: 8, z: 8, core: 2. Of those that a mesh axis runs over, the one named last changes fastest.
Arguments:
- grad_up: float32 [64, 1024, 4096], P('batch', None, 'cols'), may hold values from -1.75 to 1.75
- grad_down: float32 [64, 4096, 1024], P('batch', 'cols'), may hold values from -1.75 to 1.75
- grad_query: float32 [64, 1024, 1024], P('batch', None, 'cols'), may hold values from -1.75 to 1.75
- grad_key: float32 [64, 1024, 1024], P('batch', None, 'cols'), may hold values from -1.75 to 1.75
- grad_value: float32 [64, 1024, 1024], P('batch', None, 'cols'), may hold values from -1.75 to 1.75
- grad_mixed: float32 [64, 1024, 1024], P('batch', 'cols'), may hold values from -1.75 to 1.75
- grad_norm: float32 [64, 1024], P('batch'), may hold values from -16 to 16
- weight_up: float32 [1024, 4096], P('batch', 'cols'), may hold values from -0.1875 to 0.1875
- weight_down: float32 [4096, 1024], P('cols', 'batch'), may hold values from -0.09375 to 0.09375
- weight_query: float32 [1024, 1024], P('batch', 'cols'), may hold values from -0.1875 to 0.1875
- weight_key: float32 [1024, 1024], P('batch', 'cols'), may hold values from -0.1875 to 0.1875
- weight_value: float32 [1024, 1024], P('batch', 'cols'), may hold values from -0.1875 to 0.1875
- weight_mixed: float32 [1024, 1024], P('cols', 'batch'), may hold values from -0.1875 to 0.1875
- weight_norm: float32 [1024], P('batch'), may hold values from 0.25 to 1.75
Outputs:
- copy_up: bfloat16 [1024, 4096], P(None, 'cols')
- copy_down: bfloat16 [4096, 1024], P('cols')
- copy_query: bfloat16 [1024, 1024], P(None, 'cols')
- copy_key: bfloat16 [1024, 1024], P(None, 'cols')
- copy_value: bfloat16 [1024, 1024], P(None, 'cols')
- copy_mixed: bfloat16 [1024, 1024], P('cols')
- copy_norm: bfloat16 [1024], replicated
- new_up: float32 [1024, 4096], P('batch', 'cols')
- new_down: float32 [4096, 1024], P('cols', 'batch')
- new_query: float32 [1024, 1024], P('batch', 'cols')
- new_key: float32 [1024, 1024], P('batch', 'cols')
- new_value: float32 [1024, 1024], P('batch', 'cols')
- new_mixed: float32 [1024, 1024], P('cols', 'batch')
- new_norm: float32 [1024], P('batch')
All inputs are finite; a program needn't handle non-finite values.
Results may differ from a plain program's by a relative error of at most 0.0004.
Values may be sent and summed in bfloat16 or wider, within the bound.
No kernel may reach another device: no remote copies, remote signals or barrier semaphores. Data moves between devices by JAX's collectives and lax.ppermute only.
A program may use at most 64 MiB of HBM per device.

v0:
```python
import jax
import jax.numpy as jnp
from jax import lax
from jax.sharding import PartitionSpec as P

learn_rate = 0.3


def in_blocks(x, dim, count):
    before, after = (x.shape[:dim], x.shape[dim + 1 :])
    return jnp.moveaxis(x.reshape(*before, count, -1, *after), dim, 0)


def one_scatter(arrays, axis, dims):
    count = lax.axis_size(axis)
    parts = [in_blocks(a, dim, count) for a, dim in zip(arrays, dims)]
    lines = jnp.concatenate([b.reshape(count, -1) for b in parts], axis=1)
    extent = max(16, -(-lines.shape[1] // 1024) * 8)
    lines = jnp.pad(lines, ((0, 0), (0, extent * 128 - lines.shape[1]))).reshape(-1, 128)
    flat, at, done = (lax.psum_scatter(lines, axis, tiled=True).reshape(-1), 0, [])
    for b in parts:
        part = b[0]
        done.append(flat[at : at + part.size].reshape(part.shape))
        at += part.size
    return tuple(done)


def rows_first(arrays, axis, dims):
    turned = [jnp.moveaxis(a, dim, 0) for a, dim in zip(arrays, dims)]
    widths = [t[0].size for t in turned]
    both = jnp.concatenate([t.reshape(-1, w) for t, w in zip(turned, widths)], axis=1)
    whole = lax.all_gather(both, axis, axis=0, tiled=True)
    parts = jnp.split(whole, [sum(widths[:k]) for k in range(1, len(widths))], axis=1)
    return tuple(
        (
            jnp.moveaxis(b.reshape(-1, *t.shape[1:]), 0, dim)
            for b, t, dim in zip(parts, turned, dims)
        )
    )


def shards(
    grad_up,
    grad_down,
    grad_query,
    grad_key,
    grad_value,
    grad_mixed,
    grad_norm,
    weight_up,
    weight_down,
    weight_query,
    weight_key,
    weight_value,
    weight_mixed,
    weight_norm,
):
    mean_up, mean_down, mean_query, mean_key, mean_value, mean_mixed, mean_norm = one_scatter(
        (
            grad_up[0],
            grad_down[0],
            grad_query[0],
            grad_key[0],
            grad_value[0],
            grad_mixed[0],
            grad_norm[0],
        ),
        "batch",
        (0, 1, 0, 0, 0, 1, 0),
    )
    mean_rate = lax.axis_size("batch") ** (-0.5)
    mean_up = mean_up * mean_rate
    mean_down = mean_down * mean_rate
    mean_query = mean_query * mean_rate
    mean_key = mean_key * mean_rate
    mean_value = mean_value * mean_rate
    mean_mixed = mean_mixed * mean_rate
    mean_norm = mean_norm * mean_rate
    new_up = weight_up - learn_rate * mean_up
    new_down = weight_down - learn_rate * mean_down
    new_query = weight_query - learn_rate * mean_query
    new_key = weight_key - learn_rate * mean_key
    new_value = weight_value - learn_rate * mean_value
    new_mixed = weight_mixed - learn_rate * mean_mixed
    new_norm = weight_norm - learn_rate * mean_norm
    copy_up, copy_down, copy_query, copy_key, copy_value, copy_mixed, copy_norm = rows_first(
        (
            new_up.astype(jnp.bfloat16),
            new_down.astype(jnp.bfloat16),
            new_query.astype(jnp.bfloat16),
            new_key.astype(jnp.bfloat16),
            new_value.astype(jnp.bfloat16),
            new_mixed.astype(jnp.bfloat16),
            new_norm.astype(jnp.bfloat16),
        ),
        "batch",
        (0, 1, 0, 0, 0, 1, 0),
    )
    return (
        copy_up,
        copy_down,
        copy_query,
        copy_key,
        copy_value,
        copy_mixed,
        copy_norm,
        new_up,
        new_down,
        new_query,
        new_key,
        new_value,
        new_mixed,
        new_norm,
    )


def solution(mesh):
    placed = (
        P("batch", None, "cols"),
        P("batch", "cols", None),
        P("batch", None, "cols"),
        P("batch", None, "cols"),
        P("batch", None, "cols"),
        P("batch", "cols", None),
        P("batch", None),
        P("batch", "cols"),
        P("cols", "batch"),
        P("batch", "cols"),
        P("batch", "cols"),
        P("batch", "cols"),
        P("cols", "batch"),
        P("batch"),
    )
    return jax.shard_map(
        shards,
        mesh=mesh,
        in_specs=placed,
        out_specs=(
            P(None, "cols"),
            P("cols", None),
            P(None, "cols"),
            P(None, "cols"),
            P(None, "cols"),
            P("cols", None),
            P(),
            P("batch", "cols"),
            P("cols", "batch"),
            P("batch", "cols"),
            P("batch", "cols"),
            P("batch", "cols"),
            P("cols", "batch"),
            P("batch"),
        ),
        check_vma=False,
    )
```

profile of v0, /device:TPU:4, one launch (start us, length us, event | category | flops | bytes accessed | tf_op | source)
XLA Modules:
  0.0 343.8 jit_solution(2726753529117511950)
XLA Ops:
  7.2 1.8 reshape_reshape_squeeze.12
  9.0 1.5 constant_dynamic-update-slice_fusion.6
  10.4 1.9 copy.68
  12.4 4.2 %copy.69 = f32[64,512,16]{0,2,1:T(8,128)} copy(f32[64,512,16]{1,2,0:T(8,128)S(1)} %bitcast.22) | data formatting | bytes 4194304 | tf_op jit(solution)/shard_map/transpose | solution.py:11
  16.6 2.8 copy.72
  19.4 0.9 reshape_reshape_squeeze.13
  20.3 0.9 reshape_reshape_squeeze.14
  21.2 1.9 reshape_reshape_squeeze.15
  23.1 2.0 copy.70
  25.1 1.6 copy.71
  26.7 1.1 copy.73
  29.1 1.5 constant_dynamic-update-slice_fusion.5
  30.6 1.9 constant_dynamic-update-slice_fusion.4
  32.5 1.9 constant_dynamic-update-slice_fusion.3
  34.4 0.9 constant_dynamic-update-slice_fusion.2
  35.3 0.9 constant_dynamic-update-slice_fusion.1
  36.8 6.0 %pad.4 = f32[64,25600]{1,0:T(8,128)} pad(f32[64,24592]{1,0:T(8,128)} %constant_dynamic-update-slice_fusion, f32[]{:T(128)} %constant.8.clone.1), padding=0_0x0_1008 | pad | bytes 12849156 | tf_op jit(solution)/shard_map/jit(_pad)/pad | solution.py:19
  42.8 6.4 %reshape.72 = f32[12800,128]{1,0:T(8,128)} reshape(f32[64,25600]{1,0:T(8,128)} %pad.4) | data formatting | bytes 13107200 | tf_op jit(solution)/shard_map/reshape | solution.py:19
  49.3 1.3 dynamic-slice
  51.3 184.5 %all-reduce.4.cloned.1.call-done = f32[12800,128]{1,0:T(8,128)} async-done(((f32[12800,128]{1,0:T(8,128)}), f32[12800,128]{1,0:T(8,128)}) %all-reduce.4.cloned.1.call-update) | async-done | bytes 6553616
  235.7 0.8 dynamic-slice_multiply_fusion
  236.7 0.7 dynamic-slice_multiply_fusion.2
  237.6 0.9 dynamic-slice_bitcast_fusion
  240.4 1.3 constant_dynamic-update-slice_fusion.11
  241.7 1.3 constant_dynamic-update-slice_fusion.10
  243.0 1.3 constant_dynamic-update-slice_fusion.9
  245.6 82.8 %all-gather.2.cloned.1.call-done = bf16[1024,1537]{1,0:T(8,128)(2,1)} async-done(((bf16[16,1537]{1,0:T(8,128)(2,1)}), bf16[1024,1537]{1,0:T(8,128)(2,1)}) %all-gather.2.cloned.1.call-update) | async-done | bytes 3147792 | tf_op jit(solution)/shard_map/all_gather | solution.py:32
  328.4 2.7 slice_bitcast_fusion
  331.0 1.3 copy.77
  332.3 2.1 slice_bitcast_fusion.1
  334.4 0.8 copy.78
  335.3 1.7 slice_reduce_fusion
  (45 shorter events, 5.5 us)
Async XLA Ops:
  7.2 228.5 %all-reduce.4.cloned.1.call-start = ((), (), s32[]{:S(2)}) async-start(), calls=%async_computation.1 | async-start | bytes 13107200
  12.4 7.1 %copy-start.2 = (f32[1,1024,128]{2,1,0:T(8,128)S(1)}, f32[1,1024,128]{2,1,0:T(8,128)}, u32[]{:S(2)}) copy-start(f32[1,1024,128]{2,1,0:T(8,128)} %param.16) | copy-start | bytes 1572868
  12.4 7.9 %copy-start.3 = (f32[1,1024,128]{2,1,0:T(8,128)S(1)}, f32[1,1024,128]{2,1,0:T(8,128)}, u32[]{:S(2)}) copy-start(f32[1,1024,128]{2,1,0:T(8,128)} %param.17) | copy-start | bytes 1572868
  16.6 11.8 %copy-start.11 = (f32[1,1024]{1,0:T(1,128)S(1)}, f32[1,1024]{1,0:T(1,128)}, u32[]{:S(2)}) copy-start(f32[1,1024]{1,0:T(1,128)} %param.20) | copy-start | bytes 12292
  27.8 6.6 %copy-start.1 = (f32[64,2048]{1,0:T(8,128)S(1)}, f32[64,2048]{1,0:T(8,128)}, u32[]{:S(2)}) copy-start(f32[64,2048]{1,0:T(8,128)} %reshape_reshape_squeeze.15) | copy-start | bytes 1572868
  27.8 7.5 %copy-start = (f32[64,2048]{1,0:T(8,128)S(1)}, f32[64,2048]{1,0:T(8,128)}, u32[]{:S(2)}) copy-start(f32[64,2048]{1,0:T(8,128)} %copy.73) | copy-start | bytes 1572868
  49.2 189.3 %copy-start.12 = (f32[16]{0:T(128)S(1)}, f32[16]{0:T(128)}, u32[]{:S(2)}) copy-start(f32[16]{0:T(128)} %param.27) | copy-start | bytes 196
  49.2 189.9 %copy-start.5 = (f32[16,512]{1,0:T(8,128)S(1)}, f32[16,512]{1,0:T(8,128)}, u32[]{:S(2)}) copy-start(f32[16,512]{1,0:T(8,128)} %param.21) | copy-start | bytes 98308
  49.2 190.6 %copy-start.6 = (f32[512,16]{0,1:T(8,128)S(1)}, f32[512,16]{0,1:T(8,128)}, u32[]{:S(2)}) copy-start(f32[512,16]{0,1:T(8,128)} %param.22) | copy-start | bytes 98308
  49.2 191.2 %copy-start.7 = (f32[16,128]{1,0:T(8,128)S(1)}, f32[16,128]{1,0:T(8,128)}, u32[]{:S(2)}) copy-start(f32[16,128]{1,0:T(8,128)} %param.23) | copy-start | bytes 24580
  49.2 192.5 %copy-start.8 = (f32[16,128]{1,0:T(8,128)S(1)}, f32[16,128]{1,0:T(8,128)}, u32[]{:S(2)}) copy-start(f32[16,128]{1,0:T(8,128)} %param.24) | copy-start | bytes 24580
  49.2 193.8 %copy-start.9 = (f32[16,128]{1,0:T(8,128)S(1)}, f32[16,128]{1,0:T(8,128)}, u32[]{:S(2)}) copy-start(f32[16,128]{1,0:T(8,128)} %param.25) | copy-start | bytes 24580
  49.2 195.1 %copy-start.10 = (f32[128,16]{0,1:T(8,128)S(1)}, f32[128,16]{0,1:T(8,128)}, u32[]{:S(2)}) copy-start(f32[128,16]{0,1:T(8,128)} %param.26) | copy-start | bytes 24580
  49.3 279.1 %all-gather.2.cloned.1.call-start = ((), (), s32[]{:S(2)}) async-start(), calls=%async_computation | async-start | bytes 3461120 | tf_op jit(solution)/shard_map/all_gather | solution.py:32
  244.9 0.6 copy-start.4
Sparse Core Ops, SparseCore 0:
  49.4 186.2 all-reduce.3
  245.7 82.6 all-gather.1
where the time goes:
time: 345 us; the launch traced here: 344 us
  waiting for transfers between devices  267 us (77%)
  local copies, waits for them, and re-layouts  53.1 us (15%)
  between operations  14.9 us (4%)
  other arithmetic  8.46 us (2%)
    unnamed x3, waiting for transfers between devices  184 us
    all_gather x1, waiting for transfers between devices, rows_first(): whole = lax.all_gather(both, axis, axis=0, tiled=True)  82.8 us
    unnamed x38, local copies, waits for them, and re-layouts  17.1 us
  transfers between devices with their start and end apart: 2, of which 2 were waited for; matrix products, arithmetic and copies ran while one was open for 0% of the time, Pallas kernels for 0%

commit v1 on v0

--- a/solution.py
+++ b/solution.py
@@ -4,6 +4,13 @@
 from jax.sharding import PartitionSpec as P
 
 learn_rate = 0.3
+
+
+def exchange_gather(x, axis, dim):
+    size = lax.axis_size(axis)
+    tiles = jnp.stack([x for _ in range(size)])
+    tiles = lax.all_to_all(tiles, axis, split_axis=0, concat_axis=0)
+    return jnp.concatenate(tiles, axis=dim)
 
 
 def in_blocks(x, dim, count):
@@ -29,7 +36,7 @@
     turned = [jnp.moveaxis(a, dim, 0) for a, dim in zip(arrays, dims)]
     widths = [t[0].size for t in turned]
     both = jnp.concatenate([t.reshape(-1, w) for t, w in zip(turned, widths)], axis=1)
-    whole = lax.all_gather(both, axis, axis=0, tiled=True)
+    whole = exchange_gather(both, axis, 0)
     parts = jnp.split(whole, [sum(widths[:k]) for k in range(1, len(widths))], axis=1)
     return tuple(
         (

time: 345 us -> 349 us (1.012)
  the two profiles are of different devices: /device:TPU:4 before, /device:TPU:24 now
where the time goes in v1:
time: 349 us; the launch traced here: 348 us
  waiting for transfers between devices  184 us (53%)
  blocking collectives  90.9 us (26%)
  local copies, waits for them, and re-layouts  49.2 us (14%)
  between operations  14.8 us (4%)
  other arithmetic  8.46 us (2%)
    unnamed x2, waiting for transfers between devices  184 us
    all_to_all x1, blocking collectives, exchange_gather(): tiles = lax.all_to_all(tiles, axis, split_axis=0, concat_axis=0)  90.9 us
    unnamed x36, local copies, waits for them, and re-layouts  16.5 us
  transfers between devices with their start and end apart: 1, of which 1 were waited for; matrix products, arithmetic and copies ran while one was open for 0% of the time, Pallas kernels for 0%

profile of v1, /device:TPU:24, one launch (start us, length us, event | category | flops | bytes accessed | tf_op | source)
XLA Modules:
  0.0 347.6 jit_solution(3052250319523237695)
XLA Ops:
  7.2 1.8 reshape_reshape_squeeze.12
  9.0 1.5 constant_dynamic-update-slice_fusion.6
  10.5 1.9 copy.70
  12.5 4.2 %copy.71 = f32[64,512,16]{0,2,1:T(8,128)} copy(f32[64,512,16]{1,2,0:T(8,128)S(1)} %bitcast.26) | data formatting | bytes 4194304 | tf_op jit(solution)/shard_map/transpose | solution.py:18
  16.7 2.8 copy.74
  19.5 0.9 reshape_reshape_squeeze.13
  20.4 0.9 reshape_reshape_squeeze.14
  21.3 1.9 reshape_reshape_squeeze.15
  23.2 2.0 copy.72
  25.3 1.6 copy.73
  26.8 1.1 copy.75
  29.2 1.5 constant_dynamic-update-slice_fusion.5
  30.7 1.9 constant_dynamic-update-slice_fusion.4
  32.6 1.9 constant_dynamic-update-slice_fusion.3
  34.5 0.9 constant_dynamic-update-slice_fusion.2
  35.3 0.9 constant_dynamic-update-slice_fusion.1
  36.9 6.0 %pad.4 = f32[64,25600]{1,0:T(8,128)} pad(f32[64,24592]{1,0:T(8,128)} %constant_dynamic-update-slice_fusion, f32[]{:T(128)} %constant.8.clone.1), padding=0_0x0_1008 | pad | bytes 12849156 | tf_op jit(solution)/shard_map/jit(_pad)/pad | solution.py:26
  42.9 6.4 %reshape.77 = f32[12800,128]{1,0:T(8,128)} reshape(f32[64,25600]{1,0:T(8,128)} %pad.4) | data formatting | bytes 13107200 | tf_op jit(solution)/shard_map/reshape | solution.py:26
  49.3 1.3 dynamic-slice
  51.3 184.2 %all-reduce.4.cloned.1.call-done = f32[12800,128]{1,0:T(8,128)} async-done(((f32[12800,128]{1,0:T(8,128)}), f32[12800,128]{1,0:T(8,128)}) %all-reduce.4.cloned.1.call-update) | async-done | bytes 6553616
  235.4 0.8 dynamic-slice_multiply_fusion
  236.5 0.7 dynamic-slice_multiply_fusion.2
  237.3 0.9 dynamic-slice_bitcast_fusion
  240.1 1.3 constant_dynamic-update-slice_fusion.11
  241.4 1.3 constant_dynamic-update-slice_fusion.10
  242.7 1.3 constant_dynamic-update-slice_fusion.9
  244.9 90.9 %all_to_all.5 = bf16[64,16,1537]{2,1,0:T(8,128)(2,1)S(1)} all-to-all(bf16[64,16,1537]{2,1,0:T(8,128)(2,1)S(1)} %stack.2), channel_id=1, replica_groups=mesh['batch'=64,'cols'=8] {'batch'}, dimensions={0} | all-to-all | bytes 6295552 | tf_op jit(solution)/shard_map/all_to_all | solution.py:12
  335.8 1.1 slice_bitcast_fusion
  336.9 1.0 slice_bitcast_fusion.1
  337.9 0.7 slice_reduce_fusion
  338.6 1.3 copy.79
  339.9 0.8 copy.80
  (42 shorter events, 5.0 us)
Async XLA Ops:
  7.2 228.3 %all-reduce.4.cloned.1.call-start = ((), (), s32[]{:S(2)}) async-start(), calls=%async_computation.1 | async-start | bytes 13107200
  12.4 7.1 %copy-start.2 = (f32[1,1024,128]{2,1,0:T(8,128)S(1)}, f32[1,1024,128]{2,1,0:T(8,128)}, u32[]{:S(2)}) copy-start(f32[1,1024,128]{2,1,0:T(8,128)} %param.16) | copy-start | bytes 1572868
  12.5 8.0 %copy-start.3 = (f32[1,1024,128]{2,1,0:T(8,128)S(1)}, f32[1,1024,128]{2,1,0:T(8,128)}, u32[]{:S(2)}) copy-start(f32[1,1024,128]{2,1,0:T(8,128)} %param.17) | copy-start | bytes 1572868
  16.7 11.8 %copy-start.10 = (f32[1,1024]{1,0:T(1,128)S(1)}, f32[1,1024]{1,0:T(1,128)}, u32[]{:S(2)}) copy-start(f32[1,1024]{1,0:T(1,128)} %param.20) | copy-start | bytes 12292
  28.0 6.5 %copy-start.1 = (f32[64,2048]{1,0:T(8,128)S(1)}, f32[64,2048]{1,0:T(8,128)}, u32[]{:S(2)}) copy-start(f32[64,2048]{1,0:T(8,128)} %reshape_reshape_squeeze.15) | copy-start | bytes 1572868
  28.0 7.4 %copy-start = (f32[64,2048]{1,0:T(8,128)S(1)}, f32[64,2048]{1,0:T(8,128)}, u32[]{:S(2)}) copy-start(f32[64,2048]{1,0:T(8,128)} %copy.75) | copy-start | bytes 1572868
  49.3 189.0 %copy-start.11 = (f32[16]{0:T(128)S(1)}, f32[16]{0:T(128)}, u32[]{:S(2)}) copy-start(f32[16]{0:T(128)} %param.27) | copy-start | bytes 196
  49.3 189.6 %copy-start.4 = (f32[16,512]{1,0:T(8,128)S(1)}, f32[16,512]{1,0:T(8,128)}, u32[]{:S(2)}) copy-start(f32[16,512]{1,0:T(8,128)} %param.21) | copy-start | bytes 98308
  49.3 190.2 %copy-start.5 = (f32[512,16]{0,1:T(8,128)S(1)}, f32[512,16]{0,1:T(8,128)}, u32[]{:S(2)}) copy-start(f32[512,16]{0,1:T(8,128)} %param.22) | copy-start | bytes 98308
  49.3 190.9 %copy-start.6 = (f32[16,128]{1,0:T(8,128)S(1)}, f32[16,128]{1,0:T(8,128)}, u32[]{:S(2)}) copy-start(f32[16,128]{1,0:T(8,128)} %param.23) | copy-start | bytes 24580
  49.3 192.2 %copy-start.7 = (f32[16,128]{1,0:T(8,128)S(1)}, f32[16,128]{1,0:T(8,128)}, u32[]{:S(2)}) copy-start(f32[16,128]{1,0:T(8,128)} %param.24) | copy-start | bytes 24580
  49.3 193.5 %copy-start.8 = (f32[16,128]{1,0:T(8,128)S(1)}, f32[16,128]{1,0:T(8,128)}, u32[]{:S(2)}) copy-start(f32[16,128]{1,0:T(8,128)} %param.25) | copy-start | bytes 24580
  49.3 194.8 %copy-start.9 = (f32[128,16]{0,1:T(8,128)S(1)}, f32[128,16]{0,1:T(8,128)}, u32[]{:S(2)}) copy-start(f32[128,16]{0,1:T(8,128)} %param.26) | copy-start | bytes 24580
Sparse Core Ops, SparseCore 0:
  49.4 185.9 all-reduce.3
